TPU v7x, 32 devices: a whole 2x2x4 slice. The times are simulated.
32 devices in a mesh: ctx: 8 (over y, x, core), head: 4 (over z).
Axes of the slice: x: 2, y: 2, z: 4, core: 2. Of those that a mesh axis runs over, the one named last changes fastest.
Arguments:
- tokens: bfloat16 [1024, 4096], P('ctx'), may hold values from -8 to 8
- w_query: bfloat16 [4096, 4096], P(None, 'head'), may hold values from -1 to 1
- w_key: bfloat16 [4096, 1024], P(None, 'head'), may hold values from -1 to 1
- w_value: bfloat16 [4096, 1024], P(None, 'head'), may hold values from -0.09375 to 0.09375
- w_out: bfloat16 [4096, 4096], P('head'), may hold values from -0.09375 to 0.09375
- doc_ids: int32 [1024], P('ctx'), may hold values from 0 to 7, never falling along the last dimension, each value on 1 to 640 neighbouring positions
Outputs:
- mixed: bfloat16 [1024, 4096], P('ctx', 'head')
Inputs may be any that keep to these rules, and one draw needn't show every extreme that they name: doc_ids never fall along the context; each document has 1 to 640 tokens and one has exactly 640.
All inputs are finite; a program needn't handle non-finite values.
Results may differ from a plain program's by a relative error of at most 0.011.
Values may be sent and summed in bfloat16 or wider, within the bound.
A program may use at most 128 MiB of HBM per device.

v0:
```python
import math
import jax
import jax.numpy as jnp
from jax import lax
from jax.sharding import PartitionSpec as P

HD = 128


def rotate(vectors, places):
    half_dim = vectors.shape[-1] // 2
    freqs = 500000.0 ** (-2.0 * jnp.arange(half_dim, dtype=jnp.float32) / vectors.shape[-1])
    angles = places.astype(jnp.float32)[:, None] * freqs[None, :]
    cosine = jnp.cos(angles)[:, None, :]
    sine = jnp.sin(angles)[:, None, :]
    first_half = vectors[..., :half_dim]
    second_half = vectors[..., half_dim:]
    return jnp.concatenate(
        [first_half * cosine - second_half * sine, second_half * cosine + first_half * sine],
        axis=-1,
    )


def shards(tokens, w_query, w_key, w_value, w_out, doc_ids):
    tok_rows = tokens.shape[0]
    my_index = lax.axis_index("ctx")
    first_row = my_index * tok_rows
    places = first_row + jnp.arange(tok_rows, dtype=jnp.int32)
    query_heads = w_query.shape[1] // HD
    kv_heads = w_key.shape[1] // HD
    group_size = query_heads // kv_heads
    queries = rotate(
        jnp.dot(tokens, w_query, preferred_element_type=jnp.float32).reshape(
            tok_rows, query_heads, HD
        ),
        places,
    ).astype(jnp.bfloat16)
    queries = queries.reshape(tok_rows, kv_heads, group_size, HD)
    keys_here = rotate(
        jnp.dot(tokens, w_key, preferred_element_type=jnp.float32).reshape(tok_rows, kv_heads, HD),
        places,
    ).astype(jnp.bfloat16)
    values_here = jnp.dot(tokens, w_value, preferred_element_type=jnp.float32).astype(jnp.bfloat16)
    kv_width = kv_heads * HD
    packed = jnp.concatenate([keys_here.reshape(tok_rows, kv_width), values_here], axis=1)
    all_docs = lax.all_gather(doc_ids, "ctx", axis=0, tiled=True)
    query_low = jnp.min(doc_ids)
    query_high = jnp.max(doc_ids)
    query_last = first_row + tok_rows - 1
    score_scale = 1.0 / math.sqrt(HD)
    initial = (
        jnp.full((kv_heads, group_size, tok_rows), -1e30, jnp.float32),
        jnp.zeros((kv_heads, group_size, tok_rows), jnp.float32),
        jnp.zeros((kv_heads, group_size, tok_rows, HD), jnp.float32),
    )
    block_kv = lax.all_gather(packed, "ctx", axis=0, tiled=True)
    key_start = jnp.int32(0)
    key_count = block_kv.shape[0]
    key_start = jnp.asarray(key_start, jnp.int32)
    key_index = jnp.arange(key_count, dtype=jnp.int32)

    def accumulate(inner):
        run_max, run_sum, run_acc = inner
        block_keys = block_kv[:, :kv_width].reshape(key_count, kv_heads, HD)
        block_values = block_kv[:, kv_width:].reshape(key_count, kv_heads, HD)
        allowed = (all_docs[None, :] == doc_ids[:, None]) & (key_index[None, :] <= places[:, None])
        scores = (
            jnp.einsum("tjgd,njd->jgtn", queries, block_keys, preferred_element_type=jnp.float32)
            * score_scale
        )
        scores = jnp.where(allowed, scores, -1e30)
        new_max = jnp.maximum(run_max, jnp.max(scores, axis=-1))
        weights = jnp.exp(scores - new_max[..., None]) * allowed.astype(jnp.float32)
        new_sum = jnp.sum(weights, axis=-1)
        summed = jnp.einsum(
            "jgtn,njd->jgtd",
            weights.astype(jnp.bfloat16),
            block_values,
            preferred_element_type=jnp.float32,
        )
        return (new_max, new_sum, summed)

    touches = (
        (jnp.max(all_docs) >= query_low)
        & (jnp.min(all_docs) <= query_high)
        & (key_start <= query_last)
        & (key_start >= 0)
    )
    state = lax.cond(touches, accumulate, lambda inner: inner, initial)
    run_max, run_sum, run_acc = state
    result = run_acc / run_sum[..., None]
    attended = (
        jnp.transpose(result, (2, 0, 1, 3)).reshape(tok_rows, query_heads * HD).astype(jnp.bfloat16)
    )
    partial_value = jnp.dot(attended, w_out, preferred_element_type=jnp.float32)
    return lax.psum_scatter(
        partial_value.astype(jnp.bfloat16), "head", scatter_dimension=1, tiled=True
    )


def solution(mesh):
    return jax.shard_map(
        shards,
        mesh=mesh,
        in_specs=(
            P("ctx", None),
            P(None, "head"),
            P(None, "head"),
            P(None, "head"),
            P("head", None),
            P("ctx"),
        ),
        out_specs=P("ctx", "head"),
        check_vma=False,
    )
```

profile of v0, /device:TPU:0, one launch (start us, length us, event | category | flops | bytes accessed | tf_op | source)
XLA Modules:
  0.0 87.9 jit_solution(16131842945093330449)
XLA Ops:
  6.5 0.0 copy-start
  6.6 1.6 %copy-done = bf16[4096,256]{1,0:T(8,128)(2,1)S(1)} copy-done((bf16[4096,256]{1,0:T(8,128)(2,1)S(1)}, bf16[4096,256]{1,0:T(8,128)(2,1)}, u32[]{:S(2)}) %copy-start) | copy-done | bytes 2097176
  8.1 1.7 %convolution_convert_fusion.1 = bf16[128,256]{1,0:T(8,128)(2,1)S(1)} fusion(bf16[128,4096]{1,0:T(8,128)(2,1)} %param.8, bf16[4096,256]{1,0:T(8,128)(2,1)S(1)} %copy-done), kind=kOutput, calls=%fused_computation.15 | convolution fusion | flops 268468224 | bytes 3211264 | tf_op jit(solution)/shard_map/dot_general | solution.py:43
  9.8 2.4 %fusion.12 = f32[128,256]{1,0:T(8,128)S(1)} fusion(bf16[128,4096]{1,0:T(8,128)(2,1)} %param.8, bf16[4096,256]{1,0:T(8,128)(2,1)} %param.10), kind=kOutput, calls=%fused_computation.32 | convolution fusion | flops 268435456 | bytes 3276800 | tf_op jit(solution)/shard_map/dot_general | solution.py:40
  12.2 0.1 reshape.135
  12.3 0.3 multiply_cosine_fusion
  12.6 0.3 subtract_convert_fusion.1
  12.9 0.2 pad_maximum_fusion.2
  13.1 0.7 pad_maximum_fusion.1
  13.7 0.0 all-gather.3.cloned.1.call-update
  13.8 0.0 reduce-scatter.2.cloned.1.call-start
  13.8 0.0 copy-done.3
  13.8 10.3 %all-gather = s32[8,1,128]{2,1,0:T(1,128)S(1)} all-gather(s32[1,1,128]{2,1,0:T(1,128)S(1)} %bitcast.55), channel_id=1, replica_groups=mesh['ctx'=8,'head'=4] {'ctx'}, dimensions={0}, use_global_device_ids=true | all-gather | bytes 4608 | tf_op jit(solution)/shard_map/all_gather | solution.py:46
  24.1 0.7 fusion.10
  24.8 0.7 fusion.9
  28.1 4.6 %convolution_bitcast_fusion = f32[16,8,8,128]{3,1,2,0:T(8,128)S(1)} fusion(bf16[128,4096]{1,0:T(8,128)(2,1)S(1)} %copy-done.1, bf16[4096,1024]{1,0:T(8,128)(2,1)} %param.9), kind=kOutput, calls=%fused_computation.14 | convolution fusion | flops 1073741824 | bytes 9961472 | tf_op jit(solution)/shard_map/dot_general | solution.py:33
  32.7 0.1 copy.34
  32.8 0.3 subtract_convert_fusion
  33.2 0.1 pad_maximum_fusion
  33.3 6.7 %all-gather.3.cloned.1.call-done = bf16[1024,512]{1,0:T(8,128)(2,1)} async-done(((bf16[128,512]{1,0:T(8,128)(2,1)}), bf16[1024,512]{1,0:T(8,128)(2,1)}) %all-gather.3.cloned.1.call-update) | async-done | bytes 1048592 | tf_op jit(solution)/shard_map/all_gather | solution.py:56
  40.1 6.8 %conditional.1 = (f32[2,4,128]{2,1,0:T(4,128)S(1)}, f32[2,4,128,128]{2,3,1,0:T(8,128)}) conditional(s32[]{:T(128)} %convert_element_type.43, () %tuple.13, (s32[1024]{0:T(1024)S(1)}, s32[128]{0:T(128)S(1)}, s32[1024]{0:T(1024)S(1)}, s32[]{:T(128)}, s32[128]{0:T(128)S(1)}, /*index=5*/bf16[1024,512]{1,0:T(8,128)(2,1)}, ...), branch_computations={%region_4.0_spmd, %region_5.8_spmd} | conditional | flops 551025792 | bytes 22841392 | solution.py:89
  40.1 1.2 %compare_and_fusion = (pred[128,1024]{0,1:T(8,128)(4,1)S(1)}, f32[128,1024]{0,1:T(8,128)}) fusion(s32[128]{0:T(128)S(1)} %broadcast_add_fusion, s32[128]{0:T(128)S(1)} %get-tuple-element.22, s32[1024]{0:T(1024)S(1)} %get-tuple-element.23, s32[1024]{0:T(1024)S(1)} %get-tuple-element.21), kind=kLoop, calls=%fused_computation.7 | loop fusion | flops 524288 | bytes 664576 | tf_op jit(solution)/shard_map/cond/branch_1_fun/and | solution.py:66
  41.2 1.5 %copy.22 = bf16[1024,512]{0,1:T(8,128)(2,1)S(1)} copy(bf16[1024,512]{1,0:T(8,128)(2,1)} %get-tuple-element.44) | data formatting | bytes 2097152 | tf_op jit(solution)/shard_map
  42.7 0.1 fusion.11
  42.8 0.9 fusion
  43.7 0.1 copy-done.2
  43.8 2.1 %fusion.3 = f32[2,4,128,128]{2,3,1,0:T(8,128)} fusion(bf16[1024,2,128,1]{0,2,3,1:T(8,128)(2,1)S(1)} %bitcast.51, f32[2,1024,128,4]{2,1,3,0:T(8,128)S(1)} %get-tuple-element.56, f32[128,1024]{0,1:T(8,128)S(1)} %copy-done.2, f32[2,4,128]{2,1,0:T(4,128)S(1)} %broadcast_maximum_fusion, pred[128,1024]{0,1:T(8,128)(4,1)S(1)} %get-tuple-element.53), kind=kOutput, calls=%fused_computation.5 | convolution fusion | flops 273678336 | bytes 5902336 | tf_op jit(solution)/shard_map/cond | solution.py:89
  45.8 1.0 %fusion.2 = f32[2,4,128]{2,1,0:T(4,128)S(1)} fusion(f32[2,1024,128,4]{2,1,3,0:T(8,128)S(1)} %get-tuple-element.56, f32[128,1024]{0,1:T(8,128)S(1)} %copy-done.2, f32[2,4,128]{2,1,0:T(4,128)S(1)} %broadcast_maximum_fusion, pred[128,1024]{0,1:T(8,128)(4,1)S(1)} %get-tuple-element.53), kind=kLoop, calls=%fused_computation.4 | loop fusion | flops 5241856 | bytes 4857856 | tf_op jit(solution)/shard_map/cond/branch_1_fun/reduce_sum | solution.py:74
  46.9 1.1 %divide_convert_fusion = bf16[2,4,128,128]{2,3,1,0:T(8,128)(2,1)S(1)} fusion(f32[2,4,128,128]{2,3,1,0:T(8,128)} %get-tuple-element.46, f32[2,4,128]{2,1,0:T(4,128)S(1)} %get-tuple-element.31), kind=kLoop, calls=%fused_computation.16 | loop fusion | flops 262144 | bytes 790528 | tf_op jit(solution)/shard_map/convert_element_type | solution.py:93
  47.9 5.7 %convolution_convert_fusion = bf16[128,4096]{1,0:T(8,128)(2,1)} fusion(bf16[128,1024]{0,1:T(8,128)(2,1)S(1)} %bitcast.48, bf16[1024,4096]{1,0:T(8,128)(2,1)} %param.12), kind=kOutput, calls=%fused_computation.13 | convolution fusion | flops 1074266112 | bytes 9699328 | tf_op jit(solution)/shard_map/dot_general | solution.py:95
  53.6 0.0 reduce-scatter.2.cloned.1.call-update
  53.6 27.4 %reduce-scatter.2.cloned.1.call-done = bf16[128,1024]{1,0:T(8,128)(2,1)} async-done(((bf16[128,4096]{1,0:T(8,128)(2,1)}), bf16[128,1024]{1,0:T(8,128)(2,1)}) %reduce-scatter.2.cloned.1.call-update) | async-done | bytes 262160 | tf_op jit(solution)/shard_map/reduce_scatter | solution.py:96
  (14 shorter events, 0.1 us)
Async XLA Ops:
  6.5 1.6 %copy-start = (bf16[4096,256]{1,0:T(8,128)(2,1)S(1)}, bf16[4096,256]{1,0:T(8,128)(2,1)}, u32[]{:S(2)}) copy-start(bf16[4096,256]{1,0:T(8,128)(2,1)} %param.11) | copy-start | bytes 6291460
  6.5 21.5 %copy-start.1 = (bf16[128,4096]{1,0:T(8,128)(2,1)S(1)}, bf16[128,4096]{1,0:T(8,128)(2,1)}, u32[]{:S(2)}) copy-start(bf16[128,4096]{1,0:T(8,128)(2,1)} %param.8) | copy-start | bytes 3145732
  6.5 7.3 %copy-start.3 = (s32[128]{0:T(128)S(1)}, s32[128]{0:T(128)}, u32[]{:S(2)}) copy-start(s32[128]{0:T(128)} %param.13) | copy-start | bytes 1540
  6.5 33.5 %all-gather.3.cloned.1.call-start = ((), (), s32[]{:S(2)}) async-start(), calls=%async_computation.1 | async-start | bytes 1179648 | tf_op jit(solution)/shard_map/all_gather | solution.py:56
  13.8 67.3 %reduce-scatter.2.cloned.1.call-start = ((), (), s32[]{:S(2)}) async-start(), calls=%async_computation.2 | async-start | bytes 1310720 | tf_op jit(solution)/shard_map/reduce_scatter | solution.py:96
  42.7 1.0 %copy-start.2 = (f32[128,1024]{0,1:T(8,128)S(1)}, f32[128,1024]{0,1:T(8,128)}, u32[]{:S(2)}) copy-start(f32[128,1024]{0,1:T(8,128)} %get-tuple-element.54) | copy-start | bytes 1572868 | tf_op jit(solution)/shard_map/cond
Sparse Core Ops, SparseCore 0:
  13.9 26.1 all-gather.2
  53.8 27.2 reduce-scatter.1
where the time goes:
time: 88.3 us; the launch traced here: 87.9 us
  waiting for transfers between devices  34.2 us (39%)
  matrix products  17.3 us (20%)
  between operations  16.1 us (18%)
  blocking collectives  10.3 us (12%)
  other arithmetic  6.54 us (7%)
  local copies, waits for them, and re-layouts  3.45 us (4%)
    reduce_scatter x1, waiting for transfers between devices, shards(): lax.psum_scatter(partial_value.astype(jnp.bfloat16), 'head', scatter_dime...  27.4 us
    all_gather x1, blocking collectives, shards(): all_docs = lax.all_gather(doc_ids, 'ctx', axis=0, tiled=True)  10.3 us
    all_gather x1, waiting for transfers between devices, shards(): block_kv = lax.all_gather(packed, 'ctx', axis=0, tiled=True)  6.74 us
    dot_general x1, matrix products, shards(): partial_value = jnp.dot(attended, w_out, preferred_element_type=jnp.float32)  5.67 us
    dot_general x1, matrix products, shards(): jnp.dot(tokens, w_query, preferred_element_type=jnp.float32)  4.63 us
    dot_general x1, matrix products, shards(): jnp.dot(tokens, w_key, preferred_element_type=jnp.float32)  2.36 us
    cond x1, matrix products, shards(): state = lax.cond(touches, accumulate, lambda inner: inner, initial)  2.09 us
  transfers between devices with their start and end apart: 2, of which 2 were waited for; matrix products, arithmetic and copies ran while one was open for 8% of the time, Pallas kernels for 0%

commit v1 on v0

--- a/solution.py
+++ b/solution.py
@@ -53,7 +53,18 @@
         jnp.zeros((kv_heads, group_size, tok_rows), jnp.float32),
         jnp.zeros((kv_heads, group_size, tok_rows, HD), jnp.float32),
     )
-    block_kv = lax.all_gather(packed, "ctx", axis=0, tiled=True)
+    dev_count = lax.axis_size("ctx")
+    k_now = sorted(((jj, (jj + 1) % dev_count) for jj in range(dev_count)))
+    block_last = packed
+    blocks_here = [block_last]
+    d = 1
+    while d < dev_count:
+        block_last = lax.ppermute(block_last, "ctx", k_now)
+        blocks_here.insert(0, block_last)
+        d += 1
+    after = jnp.concatenate(blocks_here, 0)
+    ready = lax.axis_index("ctx")
+    block_kv = jnp.roll(after, shift=(ready + 1) * packed.shape[0], axis=0)
     key_start = jnp.int32(0)
     key_count = block_kv.shape[0]
     key_start = jnp.asarray(key_start, jnp.int32)

time: 88.3 us -> 118 us (1.34)
  waiting for transfers between devices: 34.2 us -> 50.5 us
  local copies, waits for them, and re-layouts: 3.45 us -> 18.9 us
  matrix products: 17.3 us -> 14.6 us
    ppermute x0 -> x7, waiting for transfers between devices: none -> 23.4 us  [shards(): block_last = lax.ppermute(block_last, 'ctx', k_now)]
    unnamed x8 -> x48, local copies, waits for them, and re-layouts: 1.68 us -> 13.1 us
    all_gather x1 -> x0, waiting for transfers between devices: 6.74 us -> none  [shards(): block_kv = lax.all_gather(packed, 'ctx', axis=0, tiled=True)]
    another operation x3, local copies, waits for them, and re-layouts: 1.56 us -> 4.05 us
    dot_general x1, matrix products: 2.36 us -> 0.44 us  [shards(): jnp.dot(tokens, w_key, preferred_element_type=jnp.float32)]
    slice x1, local copies, waits for them, and re-layouts: 0.07 us -> 1.76 us  [accumulate(): block_values = block_kv[:, kv_width:].reshape(key_count, kv_heads, HD)]
  transfers between devices with their start and end apart: 2 -> 8, of which waited for: 2 -> 7; matrix products, arithmetic and copies ran while one was open for 8% -> 6% of each run, Pallas kernels for 0% -> 0%
where the time goes in v1:
time: 118 us; the launch traced here: 117 us
  waiting for transfers between devices  50.5 us (43%)
  local copies, waits for them, and re-layouts  18.9 us (16%)
  between operations  16.3 us (14%)
  matrix products  14.6 us (12%)
  blocking collectives  10.5 us (9%)
  other arithmetic  5.42 us (5%)
    reduce_scatter x1, waiting for transfers between devices, shards(): lax.psum_scatter(partial_value.astype(jnp.bfloat16), 'head', scatter_dime...  27.1 us
    ppermute x7, waiting for transfers between devices, shards(): block_last = lax.ppermute(block_last, 'ctx', k_now)  23.4 us
    unnamed x48, local copies, waits for them, and re-layouts  13.1 us
    all_gather x1, blocking collectives, shards(): all_docs = lax.all_gather(doc_ids, 'ctx', axis=0, tiled=True)  10.5 us
    dot_general x1, matrix products, shards(): partial_value = jnp.dot(attended, w_out, preferred_element_type=jnp.float32)  5.66 us
    dot_general x1, matrix products, shards(): jnp.dot(tokens, w_query, preferred_element_type=jnp.float32)  4.63 us
    another operation x3, local copies, waits for them, and re-layouts  4.05 us
  transfers between devices with their start and end apart: 8, of which 7 were waited for; matrix products, arithmetic and copies ran while one was open for 6% of the time, Pallas kernels for 0%

profile of v1, /device:TPU:0, one launch (start us, length us, event | category | flops | bytes accessed | tf_op | source)
XLA Modules:
  0.0 117.2 jit_solution(8784656012841685982)
XLA Ops:
  6.6 1.5 %copy-done = bf16[4096,256]{1,0:T(8,128)(2,1)S(1)} copy-done((bf16[4096,256]{1,0:T(8,128)(2,1)S(1)}, bf16[4096,256]{1,0:T(8,128)(2,1)}, u32[]{:S(2)}) %copy-start) | copy-done | bytes 2097176
  8.1 1.7 %convolution_convert_fusion.1 = bf16[128,256]{1,0:T(8,128)(2,1)S(1)} fusion(bf16[128,4096]{1,0:T(8,128)(2,1)} %param.8, bf16[4096,256]{1,0:T(8,128)(2,1)S(1)} %copy-done), kind=kOutput, calls=%fused_computation.16 | convolution fusion | flops 268468224 | bytes 3211264 | tf_op jit(solution)/shard_map/dot_general | solution.py:43
  11.8 5.5 %collective-permute-done = bf16[128,512]{1,0:T(8,128)(2,1)S(1)} collective-permute-done((bf16[128,512]{1,0:T(8,128)(2,1)S(1)}, bf16[128,512]{1,0:T(8,128)(2,1)S(1)}, u32[]{:S(2)}, u32[]{:S(2)}) %collective-permute-start) | collective-permute-done | bytes 131104 | tf_op jit(solution)/shard_map/ppermute | solution.py:62
  17.3 5.3 %collective-permute-done.1 = bf16[128,512]{1,0:T(8,128)(2,1)S(1)} collective-permute-done((bf16[128,512]{1,0:T(8,128)(2,1)S(1)}, bf16[128,512]{1,0:T(8,128)(2,1)S(1)}, u32[]{:S(2)}, u32[]{:S(2)}) %collective-permute-start.1) | collective-permute-done | bytes 131104 | tf_op jit(solution)/shard_map/ppermute | solution.py:62
  22.6 5.3 %collective-permute-done.2 = bf16[128,512]{1,0:T(8,128)(2,1)S(1)} collective-permute-done((bf16[128,512]{1,0:T(8,128)(2,1)S(1)}, bf16[128,512]{1,0:T(8,128)(2,1)S(1)}, u32[]{:S(2)}, u32[]{:S(2)}) %collective-permute-start.2) | collective-permute-done | bytes 131104 | tf_op jit(solution)/shard_map/ppermute | solution.py:62
  27.9 5.3 %collective-permute-done.3 = bf16[128,512]{1,0:T(8,128)(2,1)S(1)} collective-permute-done((bf16[128,512]{1,0:T(8,128)(2,1)S(1)}, bf16[128,512]{1,0:T(8,128)(2,1)S(1)}, u32[]{:S(2)}, u32[]{:S(2)}) %collective-permute-start.3) | collective-permute-done | bytes 131104 | tf_op jit(solution)/shard_map/ppermute | solution.py:62
  33.3 4.6 %convolution_bitcast_fusion = f32[16,8,8,128]{3,1,2,0:T(8,128)S(1)} fusion(bf16[128,4096]{1,0:T(8,128)(2,1)S(1)} %copy-done.1, bf16[4096,1024]{1,0:T(8,128)(2,1)} %param.9), kind=kOutput, calls=%fused_computation.15 | convolution fusion | flops 1073741824 | bytes 9961472 | tf_op jit(solution)/shard_map/dot_general | solution.py:33
  39.2 10.5 %all-gather = s32[8,1,128]{2,1,0:T(1,128)S(1)} all-gather(s32[1,1,128]{2,1,0:T(1,128)S(1)} %bitcast.57), channel_id=1, replica_groups=mesh['ctx'=8,'head'=4] {'ctx'}, dimensions={0}, use_global_device_ids=true | all-gather | bytes 4608 | tf_op jit(solution)/shard_map/all_gather | solution.py:46
  49.7 0.7 fusion.9
  50.8 0.7 fusion.10
  54.4 1.5 %collective-permute-done.6 = bf16[128,512]{1,0:T(8,128)(2,1)} collective-permute-done((bf16[128,512]{1,0:T(8,128)(2,1)S(1)}, bf16[128,512]{1,0:T(8,128)(2,1)}, u32[]{:S(2)}, u32[]{:S(2)}) %collective-permute-start.6) | collective-permute-done | bytes 131104 | tf_op jit(solution)/shard_map/ppermute | solution.py:62
  55.8 1.6 %constant_dynamic-update-slice_fusion.15 = bf16[2048,512]{1,0:T(8,128)(2,1)} fusion(bf16[128,512]{1,0:T(8,128)(2,1)} %collective-permute-done.6), kind=kLoop, calls=%fused_computation.43 | loop fusion | bytes 262144
  57.4 0.7 constant_dynamic-update-slice_fusion.14
  58.1 0.7 constant_dynamic-update-slice_fusion.13
  59.4 0.7 constant_dynamic-update-slice_fusion.11
  60.0 0.7 constant_dynamic-update-slice_fusion.10
  60.7 0.7 constant_dynamic-update-slice_fusion.9
  61.4 0.7 constant_dynamic-update-slice_fusion.8
  62.0 1.6 %constant_dynamic-update-slice_fusion.7 = bf16[2048,512]{1,0:T(8,128)(2,1)} fusion(bf16[2048,512]{1,0:T(8,128)(2,1)} %constant_dynamic-update-slice_fusion.8, bf16[128,512]{1,0:T(8,128)(2,1)} %collective-permute-done.6), kind=kLoop, calls=%fused_computation.35 | loop fusion | bytes 262144
  63.6 0.7 constant_dynamic-update-slice_fusion.6
  64.9 0.7 constant_dynamic-update-slice_fusion.4
  66.2 0.7 constant_dynamic-update-slice_fusion.2
  66.9 0.7 constant_dynamic-update-slice_fusion.1
  67.5 0.7 constant_dynamic-update-slice_fusion
  68.2 9.3 %conditional.1 = (f32[2,4,128]{2,1,0:T(4,128)S(1)}, f32[2,4,128,128]{2,3,1,0:T(8,128)S(1)}) conditional(s32[]{:T(128)} %convert_element_type.49, () %tuple.24, (s32[1024]{0:T(1024)S(1)}, s32[128]{0:T(128)S(1)}, s32[1024]{0:T(1024)S(1)}, s32[]{:T(128)}, s32[128]{0:T(128)S(1)}, /*index=5*/s32[]{:T(128)}, s32[]{:T(128)}, ...), branch_computations={%region_4.5_spmd, %region_5.8_spmd.clone} | conditional | flops 551025792 | bytes 22841540 | solution.py:100
  68.5 4.0 %copy.22 = bf16[2048,512]{0,1:T(8,128)(2,1)} copy(bf16[2048,512]{1,0:T(8,128)(2,1)} %get-tuple-element.183) | data formatting | bytes 4194304 | tf_op jit(solution)/shard_map
  72.5 1.8 %fusion.11 = (bf16[1024,256]{0,1:T(8,128)(2,1)S(1)}, bf16[1024,256]{0,1:T(8,128)(2,1)S(1)}) fusion(bf16[2048,512]{0,1:T(8,128)(2,1)} %copy.22, s32[]{:T(128)S(6)} %select_n.28, s32[]{:T(128)S(6)} %add.59), kind=kLoop, calls=%fused_computation.48 | loop fusion | bytes 2097160 | tf_op jit(solution)/shard_map/cond/branch_1_fun/slice | solution.py:76
  74.3 0.9 fusion
  75.2 1.3 %fusion.3 = f32[2,4,128,128]{2,3,1,0:T(8,128)S(1)} fusion(bf16[1024,2,128,1]{0,2,3,1:T(8,128)(2,1)S(1)} %bitcast.54, f32[2,1024,128,4]{2,1,3,0:T(8,128)S(1)} %get-tuple-element.199, f32[128,1024]{0,1:T(8,128)S(1)} %get-tuple-element.197, f32[2,4,128]{2,1,0:T(4,128)S(1)} %broadcast_maximum_fusion, pred[128,1024]{0,1:T(8,128)(4,1)S(1)} %get-tuple-element.196), kind=kOutput, calls=%fused_computation.5 | convolution fusion | flops 273678336 | bytes 5902336 | tf_op jit(solution)/shard_map/cond | solution.py:100
  76.5 1.0 fusion.2
  77.5 5.7 %convolution_convert_fusion = bf16[128,4096]{1,0:T(8,128)(2,1)} fusion(bf16[128,1024]{0,1:T(8,128)(2,1)S(1)} %bitcast.48, bf16[1024,4096]{1,0:T(8,128)(2,1)} %param.12), kind=kOutput, calls=%fused_computation.14 | convolution fusion | flops 1074266112 | bytes 9699328 | tf_op jit(solution)/shard_map/dot_general | solution.py:106
  83.2 27.1 %reduce-scatter.2.cloned.1.call-done = bf16[128,1024]{1,0:T(8,128)(2,1)} async-done(((bf16[128,4096]{1,0:T(8,128)(2,1)}), bf16[128,1024]{1,0:T(8,128)(2,1)}) %reduce-scatter.2.cloned.1.call-update) | async-done | bytes 262160 | tf_op jit(solution)/shard_map/reduce_scatter | solution.py:107
  (65 shorter events, 6.2 us)
Async XLA Ops:
  6.5 1.6 %copy-start = (bf16[4096,256]{1,0:T(8,128)(2,1)S(1)}, bf16[4096,256]{1,0:T(8,128)(2,1)}, u32[]{:S(2)}) copy-start(bf16[4096,256]{1,0:T(8,128)(2,1)} %param.11) | copy-start | bytes 6291460
  6.5 3.3 %copy-start.1 = (bf16[128,4096]{1,0:T(8,128)(2,1)S(1)}, bf16[128,4096]{1,0:T(8,128)(2,1)}, u32[]{:S(2)}) copy-start(bf16[128,4096]{1,0:T(8,128)(2,1)} %param.8) | copy-start | bytes 3145732
  6.5 103.8 %reduce-scatter.2.cloned.1.call-start = ((), (), s32[]{:S(2)}) async-start(), calls=%async_computation.1 | async-start | bytes 1310720 | tf_op jit(solution)/shard_map/reduce_scatter | solution.py:107
  6.6 3.3 %copy-start.2 = (bf16[4096,256]{1,0:T(8,128)(2,1)S(1)}, bf16[4096,256]{1,0:T(8,128)(2,1)}, u32[]{:S(2)}) copy-start(bf16[4096,256]{1,0:T(8,128)(2,1)} %param.10) | copy-start | bytes 6291460
  9.8 1.4 %copy-start.3 = (bf16[128,256]{1,0:T(8,128)(2,1)}, bf16[128,256]{1,0:T(8,128)(2,1)S(1)}, u32[]{:S(2)}) copy-start(bf16[128,256]{1,0:T(8,128)(2,1)S(1)} %convolution_convert_fusion.1) | copy-start | bytes 196612
  11.2 6.1 %collective-permute-start = (bf16[128,512]{1,0:T(8,128)(2,1)S(1)}, bf16[128,512]{1,0:T(8,128)(2,1)S(1)}, u32[]{:S(2)}, u32[]{:S(2)}) collective-permute-start(bf16[128,512]{1,0:T(8,128)(2,1)S(1)} %pad_maximum_fusion.1), channel_id=1, source_target_pairs={{0,4},{4,8},{8,12},{12,16},{16,20},{20,24},{24,28},{28,0},{1,5},{5... | collective-permute-start | bytes 393224 | tf_op jit(solution)/shard_map/ppermute | solution.py:62
  17.3 15.9 %copy-start.5 = (bf16[128,512]{1,0:T(8,128)(2,1)}, bf16[128,512]{1,0:T(8,128)(2,1)S(1)}, u32[]{:S(2)}) copy-start(bf16[128,512]{1,0:T(8,128)(2,1)S(1)} %collective-permute-done) | copy-start | bytes 393220
  17.3 5.3 %collective-permute-start.1 = (bf16[128,512]{1,0:T(8,128)(2,1)S(1)}, bf16[128,512]{1,0:T(8,128)(2,1)S(1)}, u32[]{:S(2)}, u32[]{:S(2)}) collective-permute-start(bf16[128,512]{1,0:T(8,128)(2,1)S(1)} %collective-permute-done), channel_id=1, source_target_pairs={{0,4},{4,8},{8,12},{12,16},{16,20},{20,24},{24,28},{28,0},{1,5},{5... | collective-permute-start | bytes 393224 | tf_op jit(solution)/shard_map/ppermute | solution.py:62
  22.6 10.6 %copy-start.7 = (bf16[128,512]{1,0:T(8,128)(2,1)}, bf16[128,512]{1,0:T(8,128)(2,1)S(1)}, u32[]{:S(2)}) copy-start(bf16[128,512]{1,0:T(8,128)(2,1)S(1)} %collective-permute-done.1) | copy-start | bytes 393220
  22.6 5.3 %collective-permute-start.2 = (bf16[128,512]{1,0:T(8,128)(2,1)S(1)}, bf16[128,512]{1,0:T(8,128)(2,1)S(1)}, u32[]{:S(2)}, u32[]{:S(2)}) collective-permute-start(bf16[128,512]{1,0:T(8,128)(2,1)S(1)} %collective-permute-done.1), channel_id=1, source_target_pairs={{0,4},{4,8},{8,12},{12,16},{16,20},{20,24},{24,28},{28,0},{1,5},{5... | collective-permute-start | bytes 393224 | tf_op jit(solution)/shard_map/ppermute | solution.py:62
  27.9 5.3 %copy-start.9 = (bf16[128,512]{1,0:T(8,128)(2,1)}, bf16[128,512]{1,0:T(8,128)(2,1)S(1)}, u32[]{:S(2)}) copy-start(bf16[128,512]{1,0:T(8,128)(2,1)S(1)} %collective-permute-done.2) | copy-start | bytes 393220
  27.9 5.3 %collective-permute-start.3 = (bf16[128,512]{1,0:T(8,128)(2,1)S(1)}, bf16[128,512]{1,0:T(8,128)(2,1)S(1)}, u32[]{:S(2)}, u32[]{:S(2)}) collective-permute-start(bf16[128,512]{1,0:T(8,128)(2,1)S(1)} %collective-permute-done.2), channel_id=1, source_target_pairs={{0,4},{4,8},{8,12},{12,16},{16,20},{20,24},{24,28},{28,0},{1,5},{5... | collective-permute-start | bytes 393224 | tf_op jit(solution)/shard_map/ppermute | solution.py:62
  33.2 4.7 %copy-start.11 = (bf16[128,512]{1,0:T(8,128)(2,1)}, bf16[128,512]{1,0:T(8,128)(2,1)S(1)}, u32[]{:S(2)}) copy-start(bf16[128,512]{1,0:T(8,128)(2,1)S(1)} %collective-permute-done.3) | copy-start | bytes 393220
  33.2 5.3 %collective-permute-start.4 = (bf16[128,512]{1,0:T(8,128)(2,1)S(1)}, bf16[128,512]{1,0:T(8,128)(2,1)S(1)}, u32[]{:S(2)}, u32[]{:S(2)}) collective-permute-start(bf16[128,512]{1,0:T(8,128)(2,1)S(1)} %collective-permute-done.3), channel_id=1, source_target_pairs={{0,4},{4,8},{8,12},{12,16},{16,20},{20,24},{24,28},{28,0},{1,5},{5... | collective-permute-start | bytes 393224 | tf_op jit(solution)/shard_map/ppermute | solution.py:62
  37.9 1.3 %copy-start.15 = (s32[128]{0:T(128)S(1)}, s32[128]{0:T(128)}, u32[]{:S(2)}) copy-start(s32[128]{0:T(128)} %param.13) | copy-start | bytes 1540
  38.5 0.7 copy-start.13
  38.5 11.9 %collective-permute-start.5 = (bf16[128,512]{1,0:T(8,128)(2,1)S(1)}, bf16[128,512]{1,0:T(8,128)(2,1)S(1)}, u32[]{:S(2)}, u32[]{:S(2)}) collective-permute-start(bf16[128,512]{1,0:T(8,128)(2,1)S(1)} %collective-permute-done.4), channel_id=1, source_target_pairs={{0,4},{4,8},{8,12},{12,16},{16,20},{20,24},{24,28},{28,0},{1,5},{5... | collective-permute-start | bytes 393224 | tf_op jit(solution)/shard_map/ppermute | solution.py:62
  38.5 20.2 %copy-start.12 = (bf16[128,512]{1,0:T(8,128)(2,1)S(1)}, bf16[128,512]{1,0:T(8,128)(2,1)}, u32[]{:S(2)}) copy-start(bf16[128,512]{1,0:T(8,128)(2,1)} %copy-done.11) | copy-start | bytes 393220
  38.5 20.8 %copy-start.10 = (bf16[128,512]{1,0:T(8,128)(2,1)S(1)}, bf16[128,512]{1,0:T(8,128)(2,1)}, u32[]{:S(2)}) copy-start(bf16[128,512]{1,0:T(8,128)(2,1)} %copy-done.9) | copy-start | bytes 393220
  38.6 21.5 %copy-start.8 = (bf16[128,512]{1,0:T(8,128)(2,1)S(1)}, bf16[128,512]{1,0:T(8,128)(2,1)}, u32[]{:S(2)}) copy-start(bf16[128,512]{1,0:T(8,128)(2,1)} %copy-done.7) | copy-start | bytes 393220
  39.2 21.5 %copy-start.6 = (bf16[128,512]{1,0:T(8,128)(2,1)S(1)}, bf16[128,512]{1,0:T(8,128)(2,1)}, u32[]{:S(2)}) copy-start(bf16[128,512]{1,0:T(8,128)(2,1)} %copy-done.5) | copy-start | bytes 393220
  39.2 22.2 %copy-start.4 = (bf16[128,256]{1,0:T(8,128)(2,1)S(1)}, bf16[128,256]{1,0:T(8,128)(2,1)}, u32[]{:S(2)}) copy-start(bf16[128,256]{1,0:T(8,128)(2,1)} %copy-done.3) | copy-start | bytes 196612
  39.2 18.9 %copy-start.14 = (bf16[128,512]{1,0:T(8,128)(2,1)S(1)}, bf16[128,512]{1,0:T(8,128)(2,1)}, u32[]{:S(2)}) copy-start(bf16[128,512]{1,0:T(8,128)(2,1)} %copy-done.13) | copy-start | bytes 393220
  50.4 5.4 %collective-permute-start.6 = (bf16[128,512]{1,0:T(8,128)(2,1)S(1)}, bf16[128,512]{1,0:T(8,128)(2,1)}, u32[]{:S(2)}, u32[]{:S(2)}) collective-permute-start(bf16[128,512]{1,0:T(8,128)(2,1)S(1)} %collective-permute-done.5), channel_id=1, source_target_pairs={{0,4},{4,8},{8,12},{12,16},{16,20},{20,24},{24,28},{28,0},{1,5},{5... | collective-permute-start | bytes 393224 | tf_op jit(solution)/shard_map/ppermute | solution.py:62
Sparse Core Ops, SparseCore 0:
  83.3 26.9 reduce-scatter.1
